TPU v7x, 32 devices: a whole 2x2x4 slice. The times are simulated.
32 devices in a mesh: samp: 16 (over z, y, x), feat: 2 (over core).
Axes of the slice: x: 2, y: 2, z: 4, core: 2. Of those that a mesh axis runs over, the one named last changes fastest.
Arguments:
- design_matrix: bfloat16 [2048, 32768], P('samp', 'feat'), may hold values from -0.046875 to 0.046875
- labels: int32 [2048], P('samp'), may hold values from 0 to 1
- weights: float32 [16, 32768], P(None, ('feat', 'samp')), may hold values from -6 to 6
- lambdas: float32 [16], replicated, may hold values from 0.05 to 1
- sketch: bfloat16 [32768, 384], P(('feat', 'samp')), may hold values from -0.03125 to 0.03125
- sketch_values: float32 [384], replicated, may hold values from 0.05 to 2
Outputs:
- new_weights: float32 [16, 32768], P(None, ('feat', 'samp'))
All inputs are finite; a program needn't handle non-finite values.
Results may differ from a plain program's by a relative error of at most 0.004.
Values may be sent and summed in bfloat16 or wider, within the bound.
No kernel may reach another device: no remote copies, remote signals or barrier semaphores. Data moves between devices by JAX's collectives and lax.ppermute only.
A program may use at most 64 MiB of HBM per device.

v0:
```python
import jax
import jax.numpy as jnp
from jax import lax
from jax.sharding import PartitionSpec as P

ITERS = 2


def shards(design_matrix, labels, weights, lambdas, sketch, sketch_values):
    sketch_full = sketch.astype(jnp.float32)
    smallest = jnp.min(sketch_values)
    ratios = (smallest + lambdas[:, None]) / (sketch_values[None, :] + lambdas[:, None]) - 1.0

    def apply_rows(vector):
        vector_half = vector.astype(jnp.bfloat16)
        partial_rows = lax.dot_general(
            lax.all_gather(vector_half, "samp", axis=1, tiled=True),
            design_matrix,
            (((1,), (1,)), ((), ())),
            preferred_element_type=jnp.float32,
        )
        return lax.psum(partial_rows, "feat")

    def apply_columns(values):
        return lax.psum_scatter(
            lax.dot_general(
                design_matrix, values, (((0,), (1,)), ((), ())), preferred_element_type=jnp.float32
            ),
            "samp",
            scatter_dimension=0,
            tiled=True,
        ).T

    def precondition(residual):
        projected = jnp.dot(residual, sketch_full, precision=lax.Precision.HIGHEST)
        projected = lax.psum(projected, ("samp", "feat"))
        correction = lax.dot_general(
            ratios * projected,
            sketch_full,
            (((1,), (1,)), ((), ())),
            precision=lax.Precision.HIGHEST,
        )
        precond_res = residual + correction
        res_dot = lax.psum(jnp.sum(residual * precond_res, axis=1), ("samp", "feat"))
        return (precond_res, res_dot)

    logits = apply_rows(weights)
    probability = jax.nn.sigmoid(logits)
    hessian_diag = probability * (1.0 - probability)
    miss_rows = (probability - labels[None, :].astype(jnp.float32)).astype(jnp.bfloat16)
    gradient = apply_columns(miss_rows) + lambdas[:, None] * weights
    residual = -gradient
    precond_res, res_dot = precondition(residual)
    direction = precond_res
    update = jnp.zeros_like(residual)
    for iteration in range(ITERS):
        image_rows = apply_rows(direction)
        hess_dir = (
            apply_columns((hessian_diag * image_rows).astype(jnp.bfloat16))
            + lambdas[:, None] * direction
        )
        curvature = lax.psum(jnp.sum(direction * hess_dir, axis=1), ("samp", "feat"))
        step_size = res_dot / curvature
        update = update + step_size[:, None] * direction
        if iteration + 1 < ITERS:
            residual = residual - step_size[:, None] * hess_dir
            precond_res, new_dot = precondition(residual)
            direction = precond_res + (new_dot / res_dot)[:, None] * direction
            res_dot = new_dot
    return weights + update


def solution(mesh):
    return jax.shard_map(
        shards,
        mesh=mesh,
        in_specs=(
            P("samp", "feat"),
            P("samp"),
            P(None, ("feat", "samp")),
            P(),
            P(("feat", "samp"), None),
            P(),
        ),
        out_specs=P(None, ("feat", "samp")),
        check_vma=False,
    )
```

profile of v0, /device:TPU:10, one launch (start us, length us, event | category | flops | bytes accessed | tf_op | source)
XLA Modules:
  0.0 596.1 jit_solution(18189731865618623638)
XLA Ops:
  8.1 33.0 %all_gather.9 = bf16[16,16384]{1,0:T(8,128)(2,1)S(1)} all-gather(bf16[16,1024]{1,0:T(8,128)(2,1)S(1)} %convert_element_type.23), channel_id=1, replica_groups=mesh['samp'=16,'feat'=2] {'samp'}, dimensions={1}, use_global_device_ids=true | all-gather | bytes 557056 | tf_op jit(solution)/shard_map/all_gather | solution.py:17
  41.1 3.4 fusion.22
  44.5 2.6 psum.63
  47.1 3.8 convolution_bitcast_fusion.2
  52.3 73.3 %reduce-scatter.4.cloned.1.call-done = f32[1024,16]{0,1:T(8,128)} async-done(((f32[16384,16]{0,1:T(8,128)}), f32[1024,16]{0,1:T(8,128)}) %reduce-scatter.4.cloned.1.call-update) | async-done | bytes 65552 | tf_op jit(solution)/shard_map/reduce_scatter | solution.py:25
  125.6 0.9 fusion.2
  127.0 50.1 %psum.64 = f32[16,384]{1,0:T(8,128)S(1)} all-reduce(f32[16,384]{1,0:T(8,128)S(1)} %fusion.23), channel_id=1, replica_groups=mesh['samp'=16,'feat'=2] {'samp','feat'}, use_global_device_ids=true, to_apply=%region_3.0 | all-reduce | flops 6144 | bytes 49152 | tf_op jit(solution)/shard_map/psum | solution.py:36
  177.8 32.0 %all_gather.10 = bf16[16,16384]{1,0:T(8,128)(2,1)S(1)} all-gather(bf16[16,1024]{1,0:T(8,128)(2,1)S(1)} %get-tuple-element.9), channel_id=1, replica_groups=mesh['samp'=16,'feat'=2] {'samp'}, dimensions={1}, use_global_device_ids=true | all-gather | bytes 557056 | tf_op jit(solution)/shard_map/all_gather | solution.py:17
  209.8 3.4 fusion.24
  213.1 2.5 psum.66
  215.6 3.8 convolution_bitcast_fusion.1
  219.5 71.6 %reduce-scatter.6.cloned.1.call-done = f32[1024,16]{0,1:T(8,128)} async-done(((f32[16384,16]{0,1:T(8,128)}), f32[1024,16]{0,1:T(8,128)}) %reduce-scatter.6.cloned.1.call-update) | async-done | bytes 65552 | tf_op jit(solution)/shard_map/reduce_scatter | solution.py:25
  291.1 1.0 multiply_reduce_fusion.1
  292.1 49.7 %all-reduce = (f32[16]{0:T(128)S(1)}, f32[16]{0:T(128)S(1)}) all-reduce(f32[16]{0:T(128)S(1)} %get-tuple-element.6, f32[16]{0:T(128)S(1)} %get-tuple-element.5), channel_id=1, replica_groups=mesh['samp'=16,'feat'=2] {'samp','feat'}, use_global_device_ids=true, to_apply=%region_5.0 | all-reduce | flops 32 | bytes 256 | tf_op jit(solution)/shard_map/psum | solution.py:44
  341.9 0.9 multiply_subtract_fusion
  343.2 38.3 %psum.68 = f32[16,384]{1,0:T(8,128)S(1)} all-reduce(f32[16,384]{1,0:T(8,128)S(1)} %fusion.25), channel_id=1, replica_groups=mesh['samp'=16,'feat'=2] {'samp','feat'}, use_global_device_ids=true, to_apply=%region_10.0 | all-reduce | flops 6144 | bytes 49152 | tf_op jit(solution)/shard_map/psum | solution.py:36
  382.3 41.9 %psum.69 = f32[16]{0:T(128)S(1)} all-reduce(f32[16]{0:T(128)S(1)} %get-tuple-element.11), channel_id=1, replica_groups=mesh['samp'=16,'feat'=2] {'samp','feat'}, use_global_device_ids=true, to_apply=%region_12.0 | all-reduce | flops 16 | bytes 128 | tf_op jit(solution)/shard_map/psum | solution.py:44
  424.3 31.8 %all_gather.11 = bf16[16,16384]{1,0:T(8,128)(2,1)S(1)} all-gather(bf16[16,1024]{1,0:T(8,128)(2,1)S(1)} %fusion.20), channel_id=1, replica_groups=mesh['samp'=16,'feat'=2] {'samp'}, dimensions={1}, use_global_device_ids=true | all-gather | bytes 557056 | tf_op jit(solution)/shard_map/all_gather | solution.py:17
  456.1 3.4 fusion.26
  459.5 2.5 psum.70
  462.0 3.9 convolution_bitcast_fusion
  465.8 72.2 %reduce-scatter.8.cloned.1.call-done = f32[1024,16]{0,1:T(8,128)} async-done(((f32[16384,16]{0,1:T(8,128)}), f32[1024,16]{0,1:T(8,128)}) %reduce-scatter.8.cloned.1.call-update) | async-done | bytes 65552 | tf_op jit(solution)/shard_map/reduce_scatter | solution.py:25
  538.1 1.0 fusion.1
  539.1 49.8 %psum.71 = f32[16]{0:T(128)S(1)} all-reduce(f32[16]{0:T(128)S(1)} %fusion.1), channel_id=1, replica_groups=mesh['samp'=16,'feat'=2] {'samp','feat'}, use_global_device_ids=true, to_apply=%region_16.0 | all-reduce | flops 16 | bytes 128 | tf_op jit(solution)/shard_map/psum | solution.py:62
  (27 shorter events, 6.2 us)
Async XLA Ops:
  6.5 120.0 %copy-start = (bf16[1024,384]{1,0:T(8,128)(2,1)S(1)}, bf16[1024,384]{1,0:T(8,128)(2,1)}, u32[]{:S(2)}) copy-start(bf16[1024,384]{1,0:T(8,128)(2,1)} %param.10) | copy-start | bytes 2359300
  6.5 119.1 %reduce-scatter.4.cloned.1.call-start = ((), (), s32[]{:S(2)}) async-start(), calls=%async_computation.3 | async-start | bytes 1114112 | tf_op jit(solution)/shard_map/reduce_scatter | solution.py:25
  44.4 6.6 %copy-start.3 = (f32[384]{0:T(512)S(1)}, f32[384]{0:T(512)}, u32[]{:S(2)}) copy-start(f32[384]{0:T(512)} %param.11) | copy-start | bytes 4612
  44.4 7.2 %copy-start.2 = (f32[16]{0:T(128)S(1)}, f32[16]{0:T(128)}, u32[]{:S(2)}) copy-start(f32[16]{0:T(128)} %param.9) | copy-start | bytes 196
  44.4 81.2 %copy-start.1 = (f32[16,1024]{1,0:T(8,128)S(1)}, f32[16,1024]{1,0:T(8,128)}, u32[]{:S(2)}) copy-start(f32[16,1024]{1,0:T(8,128)} %param.8) | copy-start | bytes 196612
  51.0 240.1 %reduce-scatter.6.cloned.1.call-start = ((), (), s32[]{:S(2)}) async-start(), calls=%async_computation.4 | async-start | bytes 1114112 | tf_op jit(solution)/shard_map/reduce_scatter | solution.py:25
  219.5 318.6 %reduce-scatter.8.cloned.1.call-start = ((), (), s32[]{:S(2)}) async-start(), calls=%async_computation.5 | async-start | bytes 1114112 | tf_op jit(solution)/shard_map/reduce_scatter | solution.py:25
Sparse Core Ops, SparseCore 0:
  51.1 74.4 reduce-scatter.3
  219.6 71.4 reduce-scatter.5
  466.0 72.0 reduce-scatter.7
where the time goes:
time: 597 us; the launch traced here: 596 us
  blocking collectives  334 us (56%)
  waiting for transfers between devices  217 us (36%)
  matrix products  24.1 us (4%)
  between operations  13.2 us (2%)
  other arithmetic  7.54 us (1%)
    reduce_scatter x3, waiting for transfers between devices, apply_columns(): lax.psum_scatter(lax.dot_general(design_matrix, values, (((0,), (1,)), ((...  217 us
    all_gather x3, blocking collectives, apply_rows(): lax.all_gather(vector_half, 'samp', axis=1, tiled=True)  96.7 us
    psum x2, blocking collectives, precondition(): lax.psum(jnp.sum(residual * precond_res, axis=1), ('samp', 'feat'))  91.6 us
    psum x2, blocking collectives, precondition(): projected = lax.psum(projected, ('samp', 'feat'))  88.3 us
    psum x1, blocking collectives, shards(): lax.psum(jnp.sum(direction * hess_dir, axis=1), ('samp', 'feat'))  49.8 us
  transfers between devices with their start and end apart: 3, of which 3 were waited for; matrix products, arithmetic and copies ran while one was open for 0% of the time, Pallas kernels for 0%

commit v1 on v0

--- a/solution.py
+++ b/solution.py
@@ -14,7 +14,7 @@
     def apply_rows(vector):
         vector_half = vector.astype(jnp.bfloat16)
         partial_rows = lax.dot_general(
-            lax.all_gather(vector_half, "samp", axis=1, tiled=True),
+            jnp.concatenate(lax.all_gather(vector_half, "samp"), axis=1),
             design_matrix,
             (((1,), (1,)), ((), ())),
             preferred_element_type=jnp.float32,

time: 597 us -> 597 us (level)
  no operation moved by 1% of the time
where the time goes in v1:
time: 597 us; the launch traced here: 596 us
  blocking collectives  334 us (56%)
  waiting for transfers between devices  217 us (36%)
  matrix products  24.1 us (4%)
  between operations  13.2 us (2%)
  other arithmetic  7.54 us (1%)
    reduce_scatter x3, waiting for transfers between devices, apply_columns(): lax.psum_scatter(lax.dot_general(design_matrix, values, (((0,), (1,)), ((...  217 us
    all_gather x3, blocking collectives, apply_rows(): lax.all_gather(vector_half, 'samp')  96.7 us
    psum x2, blocking collectives, precondition(): lax.psum(jnp.sum(residual * precond_res, axis=1), ('samp', 'feat'))  91.6 us
    psum x2, blocking collectives, precondition(): projected = lax.psum(projected, ('samp', 'feat'))  88.3 us
    psum x1, blocking collectives, shards(): lax.psum(jnp.sum(direction * hess_dir, axis=1), ('samp', 'feat'))  49.8 us
  transfers between devices with their start and end apart: 3, of which 3 were waited for; matrix products, arithmetic and copies ran while one was open for 0% of the time, Pallas kernels for 0%

profile of v1, /device:TPU:10, one launch (start us, length us, event | category | flops | bytes accessed | tf_op | source)
XLA Modules:
  0.0 596.2 jit_solution(17795729915163834470)
XLA Ops:
  8.1 33.0 %all-gather = bf16[256,1024]{1,0:T(8,128)(2,1)S(1)} all-gather(bf16[16,1024]{1,0:T(8,128)(2,1)S(1)} %convert_element_type.23), channel_id=2, replica_groups=mesh['samp'=16,'feat'=2] {'samp'}, dimensions={0}, use_global_device_ids=true | all-gather | bytes 557056 | tf_op jit(solution)/shard_map/all_gather | solution.py:17
  41.1 3.4 fusion.22
  44.5 2.6 psum.63
  47.1 3.8 convolution_bitcast_fusion.2
  52.3 73.3 %reduce-scatter.4.cloned.1.call-done = f32[1024,16]{0,1:T(8,128)} async-done(((f32[16384,16]{0,1:T(8,128)}), f32[1024,16]{0,1:T(8,128)}) %reduce-scatter.4.cloned.1.call-update) | async-done | bytes 65552 | tf_op jit(solution)/shard_map/reduce_scatter | solution.py:25
  125.7 0.9 fusion.2
  127.0 50.1 %psum.64 = f32[16,384]{1,0:T(8,128)S(1)} all-reduce(f32[16,384]{1,0:T(8,128)S(1)} %fusion.23), channel_id=1, replica_groups=mesh['samp'=16,'feat'=2] {'samp','feat'}, use_global_device_ids=true, to_apply=%region_3.0 | all-reduce | flops 6144 | bytes 49152 | tf_op jit(solution)/shard_map/psum | solution.py:36
  177.8 32.0 %all-gather.1 = bf16[256,1024]{1,0:T(8,128)(2,1)S(1)} all-gather(bf16[16,1024]{1,0:T(8,128)(2,1)S(1)} %get-tuple-element.9), channel_id=3, replica_groups=mesh['samp'=16,'feat'=2] {'samp'}, dimensions={0}, use_global_device_ids=true | all-gather | bytes 557056 | tf_op jit(solution)/shard_map/all_gather | solution.py:17
  209.9 3.4 fusion.24
  213.2 2.5 psum.66
  215.7 3.8 convolution_bitcast_fusion.1
  219.6 71.6 %reduce-scatter.6.cloned.1.call-done = f32[1024,16]{0,1:T(8,128)} async-done(((f32[16384,16]{0,1:T(8,128)}), f32[1024,16]{0,1:T(8,128)}) %reduce-scatter.6.cloned.1.call-update) | async-done | bytes 65552 | tf_op jit(solution)/shard_map/reduce_scatter | solution.py:25
  291.2 1.0 multiply_reduce_fusion.1
  292.2 49.7 %all-reduce = (f32[16]{0:T(128)S(1)}, f32[16]{0:T(128)S(1)}) all-reduce(f32[16]{0:T(128)S(1)} %get-tuple-element.6, f32[16]{0:T(128)S(1)} %get-tuple-element.5), channel_id=1, replica_groups=mesh['samp'=16,'feat'=2] {'samp','feat'}, use_global_device_ids=true, to_apply=%region_5.0 | all-reduce | flops 32 | bytes 256 | tf_op jit(solution)/shard_map/psum | solution.py:44
  342.0 0.9 multiply_subtract_fusion
  343.3 38.3 %psum.68 = f32[16,384]{1,0:T(8,128)S(1)} all-reduce(f32[16,384]{1,0:T(8,128)S(1)} %fusion.25), channel_id=1, replica_groups=mesh['samp'=16,'feat'=2] {'samp','feat'}, use_global_device_ids=true, to_apply=%region_10.0 | all-reduce | flops 6144 | bytes 49152 | tf_op jit(solution)/shard_map/psum | solution.py:36
  382.4 41.9 %psum.69 = f32[16]{0:T(128)S(1)} all-reduce(f32[16]{0:T(128)S(1)} %get-tuple-element.11), channel_id=1, replica_groups=mesh['samp'=16,'feat'=2] {'samp','feat'}, use_global_device_ids=true, to_apply=%region_12.0 | all-reduce | flops 16 | bytes 128 | tf_op jit(solution)/shard_map/psum | solution.py:44
  424.4 31.8 %all-gather.2 = bf16[256,1024]{1,0:T(8,128)(2,1)S(1)} all-gather(bf16[16,1024]{1,0:T(8,128)(2,1)S(1)} %fusion.20), channel_id=4, replica_groups=mesh['samp'=16,'feat'=2] {'samp'}, dimensions={0}, use_global_device_ids=true | all-gather | bytes 557056 | tf_op jit(solution)/shard_map/all_gather | solution.py:17
  456.2 3.4 fusion.26
  459.6 2.5 psum.70
  462.1 3.9 convolution_bitcast_fusion
  466.0 72.2 %reduce-scatter.8.cloned.1.call-done = f32[1024,16]{0,1:T(8,128)} async-done(((f32[16384,16]{0,1:T(8,128)}), f32[1024,16]{0,1:T(8,128)}) %reduce-scatter.8.cloned.1.call-update) | async-done | bytes 65552 | tf_op jit(solution)/shard_map/reduce_scatter | solution.py:25
  538.2 1.0 fusion.1
  539.2 49.8 %psum.71 = f32[16]{0:T(128)S(1)} all-reduce(f32[16]{0:T(128)S(1)} %fusion.1), channel_id=1, replica_groups=mesh['samp'=16,'feat'=2] {'samp','feat'}, use_global_device_ids=true, to_apply=%region_16.0 | all-reduce | flops 16 | bytes 128 | tf_op jit(solution)/shard_map/psum | solution.py:62
  (30 shorter events, 6.3 us)
Async XLA Ops:
  6.5 120.1 %copy-start = (bf16[1024,384]{1,0:T(8,128)(2,1)S(1)}, bf16[1024,384]{1,0:T(8,128)(2,1)}, u32[]{:S(2)}) copy-start(bf16[1024,384]{1,0:T(8,128)(2,1)} %param.10) | copy-start | bytes 2359300
  6.5 119.1 %reduce-scatter.4.cloned.1.call-start = ((), (), s32[]{:S(2)}) async-start(), calls=%async_computation.3 | async-start | bytes 1114112 | tf_op jit(solution)/shard_map/reduce_scatter | solution.py:25
  44.5 6.6 %copy-start.3 = (f32[384]{0:T(512)S(1)}, f32[384]{0:T(512)}, u32[]{:S(2)}) copy-start(f32[384]{0:T(512)} %param.11) | copy-start | bytes 4612
  44.5 7.2 %copy-start.2 = (f32[16]{0:T(128)S(1)}, f32[16]{0:T(128)}, u32[]{:S(2)}) copy-start(f32[16]{0:T(128)} %param.9) | copy-start | bytes 196
  44.5 81.2 %copy-start.1 = (f32[16,1024]{1,0:T(8,128)S(1)}, f32[16,1024]{1,0:T(8,128)}, u32[]{:S(2)}) copy-start(f32[16,1024]{1,0:T(8,128)} %param.8) | copy-start | bytes 196612
  51.0 240.2 %reduce-scatter.6.cloned.1.call-start = ((), (), s32[]{:S(2)}) async-start(), calls=%async_computation.4 | async-start | bytes 1114112 | tf_op jit(solution)/shard_map/reduce_scatter | solution.py:25
  219.6 318.6 %reduce-scatter.8.cloned.1.call-start = ((), (), s32[]{:S(2)}) async-start(), calls=%async_computation.5 | async-start | bytes 1114112 | tf_op jit(solution)/shard_map/reduce_scatter | solution.py:25
Sparse Core Ops, SparseCore 0:
  51.1 74.4 reduce-scatter.3
  219.7 71.4 reduce-scatter.5
  466.1 72.0 reduce-scatter.7
